TPU v7x, 32 devices: a whole 2x2x4 slice. The times are simulated.
32 devices in a mesh: rep: 2 (over x), mp: 16 (over z, y, core).
Axes of the slice: x: 2, y: 2, z: 4, core: 2. Of those that a mesh axis runs over, the one named last changes fastest.
Arguments:
- tokens: bfloat16 [1280, 3072], P(('rep', 'mp')), may hold values from -6 to 6
- w_in: bfloat16 [2, 3072, 2, 12288], P('rep', None, None, 'mp'), may hold values from -0.109375 to 0.109375
- w_down: bfloat16 [2, 12288, 3072], P('rep', 'mp'), may hold values from -0.0546875 to 0.0546875
- norm_gain: float32 [3072], replicated, may hold values from 0.1 to 1.9
- final_gain: float32 [3072], replicated, may hold values from 0.1 to 1.9
- value_head: float32 [3072], replicated, may hold values from -0.6 to 0.6
- owner: int32 [16], P('mp'), may hold values from 0 to 1
- lengths: int32 [16], P('rep'), may hold values from 20 to 80, as said below
- offsets: int32 [16], P('rep'), may hold values from 0 to 620, as said below
Outputs:
- mixed: bfloat16 [1280, 3072], P(('rep', 'mp'))
- rewards: float32 [16], P('rep')
Inputs may be any that keep to these rules, and one draw needn't show every extreme that they name: `lengths`: every rollout is at least a quarter of 80 long; in each group one rollout has exactly 80 tokens. `offsets`: rollout j of a group lies wholly within slots j * 80 to (j + 1) * 80 - 1 of its group; the other slots are padding.
All inputs are finite; a program needn't handle non-finite values.
Results may differ from a plain program's by a relative error of at most 0.0046.
Values may be sent and summed in bfloat16 or wider, within the bound.
A program may use at most 128 MiB of HBM per device.

v0:
```python
import jax
import jax.numpy as jnp
from jax import lax
from jax.sharding import PartitionSpec as P


def spread(value, axis, source):
    kept = jnp.where(lax.axis_index(axis) == source, value, 0).astype(value.dtype)
    return lax.psum(kept, axis)


def membership(slots, lengths, offsets):
    inside = (slots[:, None] >= offsets[None, :]) & (
        slots[:, None] < offsets[None, :] + lengths[None, :]
    )
    return inside.astype(jnp.float32)


def per_device(tokens, w_in, w_down, norm_gain, final_gain, value_head, owner, lengths, offsets):
    owner_index = owner[0]
    tok_rows = tokens.shape[0]
    width = tokens.shape[1]
    hidden_cols = w_in.shape[3]
    tokens_f = tokens.astype(jnp.float32)
    normed = (
        tokens_f
        * lax.rsqrt(jnp.mean(tokens_f * tokens_f, axis=1, keepdims=True) + 1e-06)
        * norm_gain
    ).astype(jnp.bfloat16)
    inner_local, outer_local = (
        spread(w_in, "rep", owner_index),
        spread(w_down, "rep", owner_index),
    )
    inner_matrix = inner_local.reshape(width, 2 * hidden_cols)
    piece = lax.all_gather(normed, "mp", axis=0, tiled=True)
    slots = jnp.arange(piece.shape[0], dtype=jnp.int32)
    row_count = piece.shape[0]
    products = jnp.dot(piece, inner_matrix, preferred_element_type=jnp.float32).reshape(
        row_count, 2, hidden_cols
    )
    gate_part = products[:, 0, :]
    up_part = products[:, 1, :]
    hidden = (
        jax.nn.gelu(gate_part, approximate=True)
        * up_part
        * jnp.sum(membership(slots, lengths, offsets), axis=1)[:, None]
    ).astype(jnp.bfloat16)
    outer_matrix = outer_local.reshape(hidden_cols, width)
    delta = lax.psum_scatter(
        jnp.dot(hidden, outer_matrix, preferred_element_type=jnp.float32),
        "mp",
        scatter_dimension=0,
        tiled=True,
    )
    resid = tokens_f + delta
    mixed = resid.astype(jnp.bfloat16)
    final = resid * lax.rsqrt(jnp.mean(resid * resid, axis=1, keepdims=True) + 1e-06) * final_gain
    values = jnp.dot(final, value_head, precision=lax.Precision.HIGHEST)
    own_slots = lax.axis_index("mp") * tok_rows + jnp.arange(tok_rows, dtype=jnp.int32)
    member = membership(own_slots, lengths, offsets)
    partial_sums = jnp.dot(values, member, precision=lax.Precision.HIGHEST)
    totals = lax.psum(partial_sums, "mp")
    rewards = totals / lengths.astype(jnp.float32)
    return (mixed, rewards)


def solution(mesh):
    in_specs = (
        P(("rep", "mp"), None),
        P("rep", None, None, "mp"),
        P("rep", "mp", None),
        P(),
        P(),
        P(),
        P("mp"),
        P("rep"),
        P("rep"),
    )
    out_specs = (P(("rep", "mp"), None), P("rep"))
    return jax.shard_map(
        per_device, mesh=mesh, in_specs=in_specs, out_specs=out_specs, check_vma=False
    )
```

profile of v0, /device:TPU:0, one launch (start us, length us, event | category | flops | bytes accessed | tf_op | source)
XLA Modules:
  0.0 530.3 jit_solution(2742017542717599871)
XLA Ops:
  8.0 0.0 all-gather.2.cloned.1.call-start
  8.1 1.1 fusion.19
  9.2 1.8 fusion.21
  10.9 0.0 all-gather.2.cloned.1.call-update
  11.0 0.0 all-reduce.3.cloned.1.call-start
  11.7 9.3 %broadcast_select_fusion = bf16[1,3072,2,768]{3,2,1,0:T(2,128)(2,1)} fusion(bf16[1,3072,2,768]{3,2,1,0:T(2,128)(2,1)} %param.10, pred[]{:T(512)S(6)} %eq.4), kind=kLoop, calls=%fused_computation | loop fusion | flops 4718592 | bytes 18874368 | tf_op jit(solution)/shard_map/jit(_where)/select_n | solution.py:8
  20.9 23.8 %copy.13 = bf16[1,3072,2,768]{1,3,2,0:T(8,128)(2,1)} copy(bf16[1,3072,2,768]{3,2,1,0:T(2,128)(2,1)} %broadcast_select_fusion) | data formatting | bytes 18874368 | tf_op jit(solution)/shard_map/reshape | solution.py:34
  44.7 2.6 select_bitcast_fusion
  47.3 0.0 all-reduce.3.cloned.1.call-update
  47.3 0.0 reduce-scatter.2.cloned.1.call-start
  47.4 0.6 copy-done.3
  47.9 0.0 copy-done.5
  48.0 0.1 convert_reduce_fusion
  48.1 15.4 %all-gather.2.cloned.1.call-done = bf16[640,3072]{1,0:T(8,128)(2,1)} async-done(((bf16[40,3072]{1,0:T(8,128)(2,1)}), bf16[640,3072]{1,0:T(8,128)(2,1)}) %all-gather.2.cloned.1.call-update) | async-done | bytes 3932176 | tf_op jit(solution)/shard_map/all_gather | solution.py:35
  63.5 311.1 %all-reduce.3.cloned.1.call-done = (bf16[768,3072]{1,0:T(8,128)(2,1)}, bf16[2,768,3072]{2,1,0:T(8,128)(2,1)}) async-done(((bf16[768,3072]{1,0:T(8,128)(2,1)}, bf16[2,768,3072]{2,1,0:T(8,128)(2,1)}), (bf16[768,3072]{1,0:T(8,128)(2,1)}, bf16[2,768,3072]{2,1,0:T(8,128)(2,1)})) %all-reduce.3.cloned.1.call-update) | async-done | bytes 14155792 | tf_op jit(solution)/shard_map/psum | solution.py:9
  374.6 10.2 %fusion = f32[640,2,768]{2,0,1:T(8,128)S(1)} fusion(bf16[2,768,3072]{2,1,0:T(8,128)(2,1)} %get-tuple-element.3, bf16[640,3072]{1,0:T(8,128)(2,1)} %all-gather.2.cloned.1.call-done), kind=kOutput, calls=%fused_computation.2 | convolution fusion | flops 6039797760 | bytes 17301504 | tf_op jit(solution)/shard_map/dot_general | solution.py:38
  384.8 6.4 %fusion.12 = f32[640,3072]{1,0:T(8,128)} fusion(bf16[768,3072]{1,0:T(8,128)(2,1)S(1)} %copy-done.4, f32[640,2,768]{2,0,1:T(8,128)S(1)} %fusion, f32[640]{0:T(1024)S(1)} %convert_reduce_fusion), kind=kOutput, calls=%fused_computation.17 | convolution fusion | flops 3025305600 | bytes 16517632 | tf_op jit(solution)/shard_map/dot_general | solution.py:50
  391.1 0.0 reduce-scatter.2.cloned.1.call-update
  391.2 95.3 %reduce-scatter.2.cloned.1.call-done = f32[40,3072]{1,0:T(8,128)} async-done(((f32[640,3072]{1,0:T(8,128)}), f32[40,3072]{1,0:T(8,128)}) %reduce-scatter.2.cloned.1.call-update) | async-done | bytes 491536 | tf_op jit(solution)/shard_map/reduce_scatter | solution.py:49
  486.5 1.9 multiply_reduce_fusion
  488.4 1.6 convolution_bitcast_fusion.1
  490.1 0.2 convolution_bitcast_fusion
  490.3 32.1 %psum.23 = f32[8]{0:T(128)S(1)} all-reduce(f32[8]{0:T(128)S(1)} %convolution_bitcast_fusion), channel_id=1, replica_groups=mesh['rep'=2,'mp'=16] {'mp'}, use_global_device_ids=true, to_apply=%region_6.7 | all-reduce | flops 8 | bytes 64 | tf_op jit(solution)/shard_map/psum | solution.py:62
  522.3 0.5 convert_divide_fusion
  (14 shorter events, 0.0 us)
Async XLA Ops:
  8.0 480.4 %copy-start = (f32[3072]{0:T(1024)S(1)}, f32[3072]{0:T(1024)}, u32[]{:S(2)}) copy-start(f32[3072]{0:T(1024)} %param.14) | copy-start | bytes 36868
  8.0 55.5 %all-gather.2.cloned.1.call-start = ((), (), s32[]{:S(2)}) async-start(), calls=%async_computation.1 | async-start | bytes 4177920 | tf_op jit(solution)/shard_map/all_gather | solution.py:35
  11.0 363.6 %all-reduce.3.cloned.1.call-start = ((), (), s32[]{:S(2)}) async-start(), calls=%async_computation.3 | async-start | bytes 28311552 | tf_op jit(solution)/shard_map/psum | solution.py:9
  47.3 0.7 copy-start.3
  47.3 0.7 copy-start.5
  47.3 439.2 %reduce-scatter.2.cloned.1.call-start = ((), (), s32[]{:S(2)}) async-start(), calls=%async_computation.2 | async-start | bytes 8355840 | tf_op jit(solution)/shard_map/reduce_scatter | solution.py:49
  374.6 10.2 %copy-start.4 = (bf16[768,3072]{1,0:T(8,128)(2,1)S(1)}, bf16[768,3072]{1,0:T(8,128)(2,1)}, u32[]{:S(2)}) copy-start(bf16[768,3072]{1,0:T(8,128)(2,1)} %get-tuple-element.2) | copy-start | bytes 14155780
  391.1 95.4 %copy-start.1 = (bf16[40,3072]{1,0:T(8,128)(2,1)S(1)}, bf16[40,3072]{1,0:T(8,128)(2,1)}, u32[]{:S(2)}) copy-start(bf16[40,3072]{1,0:T(8,128)(2,1)} %param.9) | copy-start | bytes 737284
  391.1 97.3 %copy-start.2 = (f32[3072]{0:T(1024)S(1)}, f32[3072]{0:T(1024)}, u32[]{:S(2)}) copy-start(f32[3072]{0:T(1024)} %param.13) | copy-start | bytes 36868
Sparse Core Ops, SparseCore 0:
  11.7 51.7 all-gather.1
  391.3 95.1 reduce-scatter.1
Sparse Core Ops, SparseCore 1:
  47.4 327.1 all-reduce.2
where the time goes:
time: 531 us; the launch traced here: 530 us
  waiting for transfers between devices  422 us (79%)
  blocking collectives  32.1 us (6%)
  local copies, waits for them, and re-layouts  24.4 us (5%)
  matrix products  18.4 us (3%)
  other arithmetic  17.2 us (3%)
  between operations  16.2 us (3%)
    psum x1, waiting for transfers between devices, spread(): return lax.psum(kept, axis)  311 us
    reduce_scatter x1, waiting for transfers between devices, per_device(): lax.psum_scatter(jnp.dot(hidden, outer_matrix, preferred_element_type=jnp...  95.3 us
    psum x1, blocking collectives, per_device(): totals = lax.psum(partial_sums, 'mp')  32.1 us
    reshape x1, local copies, waits for them, and re-layouts, per_device(): inner_matrix = inner_local.reshape(width, 2 * hidden_cols)  23.8 us
    all_gather x1, waiting for transfers between devices, per_device(): piece = lax.all_gather(normed, 'mp', axis=0, tiled=True)  15.4 us
  transfers between devices with their start and end apart: 3, of which 3 were waited for; matrix products, arithmetic and copies ran while one was open for 7% of the time, Pallas kernels for 0%

commit v1 on v0

--- a/solution.py
+++ b/solution.py
@@ -2,11 +2,12 @@
 import jax.numpy as jnp
 from jax import lax
 from jax.sharding import PartitionSpec as P
+from jax.lax import all_gather
 
 
 def spread(value, axis, source):
     kept = jnp.where(lax.axis_index(axis) == source, value, 0).astype(value.dtype)
-    return lax.psum(kept, axis)
+    return all_gather(kept, axis).sum(axis=0)
 
 
 def membership(slots, lengths, offsets):

time: 531 us -> 565 us (1.064)
  other arithmetic: 17.2 us -> 41.7 us
  waiting for transfers between devices: 422 us -> 436 us
    all_gather x0 -> x2, waiting for transfers between devices: none -> 328 us  [spread(): return all_gather(kept, axis).sum(axis=0)]
    psum x1 -> x0, waiting for transfers between devices: 311 us -> none  [spread(): return lax.psum(kept, axis)]
    reduce_sum x0 -> x2, other arithmetic: none -> 27.2 us  [spread(): return all_gather(kept, axis).sum(axis=0)]
    reshape x1, local copies, waits for them, and re-layouts: 23.8 us -> 8.12 us  [per_device(): inner_matrix = inner_local.reshape(width, 2 * hidden_cols)]
    dot_general x0 -> x1, local copies, waits for them, and re-layouts: none -> 12.6 us  [per_device(): jnp.dot(piece, inner_matrix, preferred_element_type=jnp.float32)]
  transfers between devices with their start and end apart: 3 -> 4, of which waited for: 3 -> 4; matrix products, arithmetic and copies ran while one was open for 7% -> 10% of each run, Pallas kernels for 0% -> 0%
where the time goes in v1:
time: 565 us; the launch traced here: 564 us
  waiting for transfers between devices  436 us (77%)
  other arithmetic  41.7 us (7%)
  blocking collectives  32.1 us (6%)
  local copies, waits for them, and re-layouts  21.6 us (4%)
  matrix products  18.3 us (3%)
  between operations  14.5 us (3%)
    all_gather x2, waiting for transfers between devices, spread(): return all_gather(kept, axis).sum(axis=0)  328 us
    reduce_scatter x1, waiting for transfers between devices, per_device(): lax.psum_scatter(jnp.dot(hidden, outer_matrix, preferred_element_type=jnp...  93.9 us
    psum x1, blocking collectives, per_device(): totals = lax.psum(partial_sums, 'mp')  32.1 us
    reduce_sum x2, other arithmetic, spread(): return all_gather(kept, axis).sum(axis=0)  27.2 us
    all_gather x1, waiting for transfers between devices, per_device(): piece = lax.all_gather(normed, 'mp', axis=0, tiled=True)  14.3 us
    dot_general x1, local copies, waits for them, and re-layouts, per_device(): jnp.dot(piece, inner_matrix, preferred_element_type=jnp.float32)  12.6 us
  transfers between devices with their start and end apart: 4, of which 4 were waited for; matrix products, arithmetic and copies ran while one was open for 10% of the time, Pallas kernels for 0%

profile of v1, /device:TPU:0, one launch (start us, length us, event | category | flops | bytes accessed | tf_op | source)
XLA Modules:
  0.0 564.4 jit_solution(12748305023824948952)
XLA Ops:
  7.9 2.5 broadcast_select_fusion
  10.4 0.0 all-gather.8.cloned.1.call-start
  10.4 8.5 %copy_select_fusion = bf16[1,3072,2,768]{3,1,2,0:T(8,128)(2,1)} fusion(bf16[1,3072,2,768]{3,2,1,0:T(2,128)(2,1)} %param.10, pred[]{:T(512)S(6)} %eq.4), kind=kLoop, calls=%fused_computation | loop fusion | flops 4718592 | bytes 18874368 | tf_op jit(solution)/shard_map/jit(_where)/select_n | solution.py:9
  19.0 0.0 all-gather.6.cloned.1.call-start
  19.1 0.9 copy-done.1
  19.9 0.2 fusion.19
  20.1 0.8 fusion.21
  20.9 0.0 reduce-scatter.2.cloned.1.call-start
  21.0 0.1 convert_reduce_fusion
  21.1 111.9 %all-gather.10.cloned.1.call-done = bf16[2,768,3072]{2,1,0:T(8,128)(2,1)} async-done(((bf16[1,768,3072]{2,1,0:T(8,128)(2,1)}), bf16[2,768,3072]{2,1,0:T(8,128)(2,1)}) %all-gather.10.cloned.1.call-update) | async-done | bytes 9437200 | tf_op jit(solution)/shard_map/all_gather | solution.py:10
  133.0 10.4 %reduce.5 = bf16[768,3072]{1,0:T(8,128)(2,1)} reduce(bf16[2,768,3072]{2,1,0:T(8,128)(2,1)} %all-gather.10.cloned.1.call-done, bf16[]{:T(256)} %constant.25.clone.1), dimensions={0}, to_apply=%region_3.4 | reduce | flops 2359296 | bytes 14155778 | tf_op jit(solution)/shard_map/reduce_sum | solution.py:10
  143.4 215.6 %all-gather.8.cloned.1.call-done = bf16[2,3072,2,768]{3,1,2,0:T(8,128)(2,1)} async-done(((bf16[1,3072,2,768]{3,1,2,0:T(8,128)(2,1)}), bf16[2,3072,2,768]{3,1,2,0:T(8,128)(2,1)}) %all-gather.8.cloned.1.call-update) | async-done | bytes 18874384 | tf_op jit(solution)/shard_map/all_gather | solution.py:10
  359.0 16.8 %reduce.4 = bf16[3072,2,768]{2,0,1:T(8,128)(2,1)} reduce(bf16[2,3072,2,768]{3,1,2,0:T(8,128)(2,1)} %all-gather.8.cloned.1.call-done, bf16[]{:T(256)} %constant.25.clone.1), dimensions={0}, to_apply=%region_1.2 | reduce | flops 4718592 | bytes 28311554 | tf_op jit(solution)/shard_map/reduce_sum | solution.py:10
  375.9 8.1 %copy.18 = bf16[2,384,8,768]{3,2,0,1:T(8,128)(2,1)} copy(bf16[2,384,8,768]{3,2,1,0:T(8,128)(2,1)} %bitcast.25) | data formatting | bytes 18874368 | tf_op jit(solution)/shard_map/reshape | solution.py:35
  384.0 12.6 %copy.16 = bf16[1536,3072]{1,0:T(8,128)(2,1)} copy(bf16[1536,3072]{0,1:T(8,128)(2,1)} %bitcast.24) | data formatting | bytes 18874368 | tf_op jit(solution)/shard_map/dot_general | solution.py:39
  396.6 14.3 %all-gather.6.cloned.1.call-done = bf16[640,3072]{1,0:T(8,128)(2,1)} async-done(((bf16[40,3072]{1,0:T(8,128)(2,1)}), bf16[640,3072]{1,0:T(8,128)(2,1)}) %all-gather.6.cloned.1.call-update) | async-done | bytes 3932176 | tf_op jit(solution)/shard_map/all_gather | solution.py:36
  411.0 10.2 %fusion = f32[640,2,768]{2,0,1:T(8,128)S(1)} fusion(bf16[2,768,3072]{2,1,0:T(8,128)(2,1)} %bitcast.26, bf16[640,3072]{1,0:T(8,128)(2,1)} %all-gather.6.cloned.1.call-done), kind=kOutput, calls=%fused_computation.2 | convolution fusion | flops 6039797760 | bytes 17301504 | tf_op jit(solution)/shard_map/dot_general | solution.py:39
  421.2 6.3 %fusion.12 = f32[640,3072]{1,0:T(8,128)} fusion(bf16[768,3072]{1,0:T(8,128)(2,1)S(1)} %bitcast.28, f32[640,2,768]{2,0,1:T(8,128)S(1)} %fusion, f32[640]{0:T(1024)S(1)} %convert_reduce_fusion), kind=kOutput, calls=%fused_computation.17 | convolution fusion | flops 3025305600 | bytes 16517632 | tf_op jit(solution)/shard_map/dot_general | solution.py:51
  427.6 93.9 %reduce-scatter.2.cloned.1.call-done = f32[40,3072]{1,0:T(8,128)} async-done(((f32[640,3072]{1,0:T(8,128)}), f32[40,3072]{1,0:T(8,128)}) %reduce-scatter.2.cloned.1.call-update) | async-done | bytes 491536 | tf_op jit(solution)/shard_map/reduce_scatter | solution.py:50
  521.5 1.9 multiply_reduce_fusion
  523.5 1.6 convolution_bitcast_fusion.1
  525.1 0.2 convolution_bitcast_fusion
  525.3 32.1 %psum.7 = f32[8]{0:T(128)S(1)} all-reduce(f32[8]{0:T(128)S(1)} %convolution_bitcast_fusion), channel_id=1, replica_groups=mesh['rep'=2,'mp'=16] {'mp'}, use_global_device_ids=true, to_apply=%region_6.7 | all-reduce | flops 8 | bytes 64 | tf_op jit(solution)/shard_map/psum | solution.py:63
  557.4 0.5 convert_divide_fusion
  (25 shorter events, 0.2 us)
Async XLA Ops:
  7.2 516.3 %copy-start = (f32[3072]{0:T(1024)S(1)}, f32[3072]{0:T(1024)}, u32[]{:S(2)}) copy-start(f32[3072]{0:T(1024)} %param.14) | copy-start | bytes 36868
  7.2 125.9 %all-gather.10.cloned.1.call-start = ((), (), s32[]{:S(2)}) async-start(), calls=%async_computation.4 | async-start | bytes 14155776 | tf_op jit(solution)/shard_map/all_gather | solution.py:10
  10.4 348.7 %all-gather.8.cloned.1.call-start = ((), (), s32[]{:S(2)}) async-start(), calls=%async_computation.3 | async-start | bytes 28311552 | tf_op jit(solution)/shard_map/all_gather | solution.py:10
  19.0 0.9 copy-start.1
  19.0 1.1 copy-start.2
  19.0 2.0 copy-start.4
  19.0 2.0 copy-start.5
  19.0 392.0 %all-gather.6.cloned.1.call-start = ((), (), s32[]{:S(2)}) async-start(), calls=%async_computation.1 | async-start | bytes 4177920 | tf_op jit(solution)/shard_map/all_gather | solution.py:36
  20.9 500.6 %reduce-scatter.2.cloned.1.call-start = ((), (), s32[]{:S(2)}) async-start(), calls=%async_computation.2 | async-start | bytes 8355840 | tf_op jit(solution)/shard_map/reduce_scatter | solution.py:50
  384.0 37.2 %slice-start = ((s8[4718592]{0:T(1024)(128)(4,1)}), s8[524288]{0:T(1024)(128)(4,1)S(1)}, s32[]{:S(2)}) async-start(s8[4718592]{0:T(1024)(128)(4,1)} %bitcast.27), calls=%async_computation.5 | async-start | bytes 1048576
  411.0 10.2 %slice-start.1 = ((s8[4718592]{0:T(1024)(128)(4,1)}), s8[4194304]{0:T(1024)(128)(4,1)S(1)}, s32[]{:S(2)}) async-start(s8[4718592]{0:T(1024)(128)(4,1)} %bitcast.27), calls=%async_computation.6 | async-start | bytes 8388608
  427.5 95.9 %copy-start.3 = (f32[3072]{0:T(1024)S(1)}, f32[3072]{0:T(1024)}, u32[]{:S(2)}) copy-start(f32[3072]{0:T(1024)} %param.13) | copy-start | bytes 36868
Sparse Core Ops, SparseCore 0:
  10.5 122.5 all-gather.9
  134.6 224.3 all-gather.7
  361.9 49.0 all-gather.5
  427.7 93.7 reduce-scatter.1

commit v2 on v0

--- a/solution.py
+++ b/solution.py
@@ -2,6 +2,7 @@
 import jax.numpy as jnp
 from jax import lax
 from jax.sharding import PartitionSpec as P
+from jax.lax import all_gather
 
 
 def spread(value, axis, source):
@@ -59,7 +60,7 @@
     own_slots = lax.axis_index("mp") * tok_rows + jnp.arange(tok_rows, dtype=jnp.int32)
     member = membership(own_slots, lengths, offsets)
     partial_sums = jnp.dot(values, member, precision=lax.Precision.HIGHEST)
-    totals = lax.psum(partial_sums, "mp")
+    totals = jnp.sum(all_gather(partial_sums, "mp"), 0)
     rewards = totals / lengths.astype(jnp.float32)
     return (mixed, rewards)
 

time: 531 us -> 532 us (level)
    psum x1 -> x0, blocking collectives: 32.1 us -> none  [per_device(): totals = lax.psum(partial_sums, 'mp')]
    unnamed x0 -> x1, blocking collectives: none -> 32.1 us
where the time goes in v2:
time: 532 us; the launch traced here: 531 us
  waiting for transfers between devices  420 us (79%)
  blocking collectives  32.1 us (6%)
  local copies, waits for them, and re-layouts  25.9 us (5%)
  matrix products  18.4 us (3%)
  other arithmetic  17.3 us (3%)
  between operations  16.9 us (3%)
    psum x1, waiting for transfers between devices, spread(): return lax.psum(kept, axis)  311 us
    reduce_scatter x1, waiting for transfers between devices, per_device(): lax.psum_scatter(jnp.dot(hidden, outer_matrix, preferred_element_type=jnp...  93.5 us
    unnamed x1, blocking collectives  32.1 us
    reshape x1, local copies, waits for them, and re-layouts, per_device(): inner_matrix = inner_local.reshape(width, 2 * hidden_cols)  23.8 us
    all_gather x1, waiting for transfers between devices, per_device(): piece = lax.all_gather(normed, 'mp', axis=0, tiled=True)  15.4 us
  transfers between devices with their start and end apart: 3, of which 3 were waited for; matrix products, arithmetic and copies ran while one was open for 7% of the time, Pallas kernels for 0%

profile of v2, /device:TPU:0, one launch (start us, length us, event | category | flops | bytes accessed | tf_op | source)
XLA Modules:
  0.0 530.7 jit_solution(16054112863221707681)
XLA Ops:
  8.0 0.0 all-gather.3.cloned.1.call-start
  8.1 1.1 fusion.19
  9.2 1.8 fusion.21
  11.0 0.0 all-reduce.4.cloned.1.call-start
  11.7 9.3 %broadcast_select_fusion = bf16[1,3072,2,768]{3,2,1,0:T(2,128)(2,1)} fusion(bf16[1,3072,2,768]{3,2,1,0:T(2,128)(2,1)} %param.10, pred[]{:T(512)S(6)} %eq.4), kind=kLoop, calls=%fused_computation | loop fusion | flops 4718592 | bytes 18874368 | tf_op jit(solution)/shard_map/jit(_where)/select_n | solution.py:9
  20.9 23.8 %copy.14 = bf16[1,3072,2,768]{1,3,2,0:T(8,128)(2,1)} copy(bf16[1,3072,2,768]{3,2,1,0:T(2,128)(2,1)} %broadcast_select_fusion) | data formatting | bytes 18874368 | tf_op jit(solution)/shard_map/reshape | solution.py:35
  44.8 2.6 select_bitcast_fusion
  47.4 0.0 reduce-scatter.2.cloned.1.call-start
  47.4 0.6 copy-done.3
  48.0 0.1 convert_reduce_fusion
  48.1 15.4 %all-gather.3.cloned.1.call-done = bf16[640,3072]{1,0:T(8,128)(2,1)} async-done(((bf16[40,3072]{1,0:T(8,128)(2,1)}), bf16[640,3072]{1,0:T(8,128)(2,1)}) %all-gather.3.cloned.1.call-update) | async-done | bytes 3932176 | tf_op jit(solution)/shard_map/all_gather | solution.py:36
  63.5 311.1 %all-reduce.4.cloned.1.call-done = (bf16[768,3072]{1,0:T(8,128)(2,1)}, bf16[2,768,3072]{2,1,0:T(8,128)(2,1)}) async-done(((bf16[768,3072]{1,0:T(8,128)(2,1)}, bf16[2,768,3072]{2,1,0:T(8,128)(2,1)}), (bf16[768,3072]{1,0:T(8,128)(2,1)}, bf16[2,768,3072]{2,1,0:T(8,128)(2,1)})) %all-reduce.4.cloned.1.call-update) | async-done | bytes 14155792 | tf_op jit(solution)/shard_map/psum | solution.py:10
  374.6 10.2 %fusion = f32[640,2,768]{2,0,1:T(8,128)S(1)} fusion(bf16[2,768,3072]{2,1,0:T(8,128)(2,1)} %get-tuple-element.3, bf16[640,3072]{1,0:T(8,128)(2,1)} %all-gather.3.cloned.1.call-done), kind=kOutput, calls=%fused_computation.2 | convolution fusion | flops 6039797760 | bytes 17301504 | tf_op jit(solution)/shard_map/dot_general | solution.py:39
  384.8 6.4 %fusion.12 = f32[640,3072]{1,0:T(8,128)} fusion(bf16[768,3072]{1,0:T(8,128)(2,1)S(1)} %copy-done.4, f32[640,2,768]{2,0,1:T(8,128)S(1)} %fusion, f32[640]{0:T(1024)S(1)} %convert_reduce_fusion), kind=kOutput, calls=%fused_computation.17 | convolution fusion | flops 3025305600 | bytes 16517632 | tf_op jit(solution)/shard_map/dot_general | solution.py:51
  391.2 0.6 copy-done.6
  391.9 0.6 dynamic-slice
  393.1 93.5 %reduce-scatter.2.cloned.1.call-done = f32[40,3072]{1,0:T(8,128)} async-done(((f32[640,3072]{1,0:T(8,128)}), f32[40,3072]{1,0:T(8,128)}) %reduce-scatter.2.cloned.1.call-update) | async-done | bytes 491536 | tf_op jit(solution)/shard_map/reduce_scatter | solution.py:50
  486.6 1.9 multiply_reduce_fusion
  488.5 1.6 convolution_bitcast_fusion.1
  490.1 0.2 convolution_bitcast_fusion
  490.3 0.2 dynamic-update-slice
  490.5 32.1 %all-reduce = f32[128]{0:T(128)S(1)} all-reduce(f32[128]{0:T(128)S(1)} %dynamic-update-slice), channel_id=2, replica_groups=mesh['rep'=2,'mp'=16] {'mp'}, use_global_device_ids=true, to_apply=%add | all-reduce | flops 128 | bytes 1024
  522.6 0.1 reshape.46
  522.7 0.5 convert_divide_fusion
  (21 shorter events, 0.1 us)
Async XLA Ops:
  8.0 480.5 %copy-start = (f32[3072]{0:T(1024)S(1)}, f32[3072]{0:T(1024)}, u32[]{:S(2)}) copy-start(f32[3072]{0:T(1024)} %param.14) | copy-start | bytes 36868
  8.0 55.5 %all-gather.3.cloned.1.call-start = ((), (), s32[]{:S(2)}) async-start(), calls=%async_computation.1 | async-start | bytes 4177920 | tf_op jit(solution)/shard_map/all_gather | solution.py:36
  11.0 363.6 %all-reduce.4.cloned.1.call-start = ((), (), s32[]{:S(2)}) async-start(), calls=%async_computation.3 | async-start | bytes 28311552 | tf_op jit(solution)/shard_map/psum | solution.py:10
  47.3 0.7 copy-start.3
  47.3 0.7 copy-start.5
  47.4 439.2 %reduce-scatter.2.cloned.1.call-start = ((), (), s32[]{:S(2)}) async-start(), calls=%async_computation.2 | async-start | bytes 8355840 | tf_op jit(solution)/shard_map/reduce_scatter | solution.py:50
  374.6 10.2 %copy-start.4 = (bf16[768,3072]{1,0:T(8,128)(2,1)S(1)}, bf16[768,3072]{1,0:T(8,128)(2,1)}, u32[]{:S(2)}) copy-start(bf16[768,3072]{1,0:T(8,128)(2,1)} %get-tuple-element.2) | copy-start | bytes 14155780
  391.2 0.7 copy-start.6
  391.2 95.4 %copy-start.1 = (bf16[40,3072]{1,0:T(8,128)(2,1)S(1)}, bf16[40,3072]{1,0:T(8,128)(2,1)}, u32[]{:S(2)}) copy-start(bf16[40,3072]{1,0:T(8,128)(2,1)} %param.9) | copy-start | bytes 737284
  391.2 97.3 %copy-start.2 = (f32[3072]{0:T(1024)S(1)}, f32[3072]{0:T(1024)}, u32[]{:S(2)}) copy-start(f32[3072]{0:T(1024)} %param.13) | copy-start | bytes 36868
Sparse Core Ops, SparseCore 0:
  11.7 51.7 all-gather.2
  391.4 95.1 reduce-scatter.1
Sparse Core Ops, SparseCore 1:
  47.4 327.1 all-reduce.3
